TPU v7x, 32 devices: a whole 2x2x4 slice. The times are simulated.
32 devices in a mesh: seq: 4 (over x, core), tensor: 8 (over z, y).
Axes of the slice: x: 2, y: 2, z: 4, core: 2. Of those that a mesh axis runs over, the one named last changes fastest.
Arguments:
- token_ids: int32 [2, 7], replicated, may hold values from 0 to 131071
- cache_lengths: int32 [7], replicated, may hold values from 1 to 5118
- embed_table: bfloat16 [131072, 1024], P('seq', 'tensor'), may hold values from -64 to 64
- attn_gain: float32 [1024], replicated, may hold values from 0.1 to 1.9
- final_gain: float32 [1024], replicated, may hold values from 0.1 to 1.9
- w_qkv: bfloat16 [1024, 3, 1024], P(None, None, 'tensor'), may hold values from -0.1875 to 0.1875
- w_out: bfloat16 [1024, 1024], P('tensor'), may hold values from -0.1875 to 0.1875
- cache_keys: bfloat16 [7, 5120, 1024], P(None, 'seq', 'tensor'), may hold values from -300 to 300
- cache_values: bfloat16 [7, 5120, 1024], P(None, 'seq', 'tensor'), may hold values from -24 to 24
Outputs:
- hidden: bfloat16 [2, 7, 1024], P(None, None, 'tensor')
- new_kv: bfloat16 [2, 2, 7, 1024], P(None, None, None, 'tensor')
- logprobs: float32 [2, 7, 131072], P(None, None, ('seq', 'tensor'))
All inputs are finite; a program needn't handle non-finite values.
Results may differ from a plain program's by a relative error of at most 0.0085.
The roundings to bfloat16 on the way count: a program that leaves them out, or rounds other values in their place, can miss the bound.
Values may be sent and summed in bfloat16 or wider, within the bound.
A program may use at most 64 MiB of HBM per device.

v0:
```python
import math
import jax
import jax.numpy as jnp
from jax import lax
from jax.sharding import PartitionSpec as P

HD = 128
epsilon = 1e-05
logit_gain = 2.0


def combined_all(value, axis, join):
    pieces = jax.tree.map(lambda part: lax.all_gather(part, axis), value)
    head = jax.tree.map(lambda part: part[0], pieces)
    tail = jax.tree.map(lambda part: part[1:], pieces)
    running, _ = lax.scan(lambda running, share: (join(running, share), None), head, tail)
    return running


def rotate(vector, positions):
    half_size = vector.shape[-1] // 2
    frequency = 10000.0 ** (-(jnp.arange(half_size, dtype=jnp.float32) * 2.0 / vector.shape[-1]))
    angles = positions.astype(jnp.float32)[..., None] * frequency
    cosine_term = jnp.cos(angles)[:, :, None, :]
    sine_term = jnp.sin(angles)[:, :, None, :]
    first_half = vector[..., :half_size]
    second_half = vector[..., half_size:]
    return jnp.concatenate(
        [
            first_half * cosine_term - second_half * sine_term,
            first_half * sine_term + second_half * cosine_term,
        ],
        -1,
    )


def pair_join(earlier, later):
    highest = jnp.maximum(earlier[0], later[0])
    return (
        highest,
        earlier[1] * jnp.exp(earlier[0] - highest) + later[1] * jnp.exp(later[0] - highest),
    )


def body(
    token_ids,
    cache_lengths,
    embed_table,
    attn_gain,
    final_gain,
    w_qkv,
    w_out,
    cache_keys,
    cache_values,
):
    streams = token_ids.shape[1]
    vocab_rows, local_width = embed_table.shape
    model_width = attn_gain.shape[0]
    heads_here = local_width // HD
    slot_count = cache_keys.shape[1]
    seq_index = lax.axis_index("seq")
    tensor_index = lax.axis_index("tensor")
    local_ids = token_ids - seq_index * vocab_rows
    inside = (local_ids >= 0) & (local_ids < vocab_rows)
    picked = embed_table[jnp.clip(local_ids, 0, vocab_rows - 1)]
    picked = jnp.where(inside[..., None], picked, jnp.zeros_like(picked))
    embed_local = lax.psum(picked.astype(jnp.float32).astype(jnp.bfloat16), "seq").astype(
        jnp.float32
    )
    embed_whole = lax.all_gather(
        embed_local.astype(jnp.bfloat16), "tensor", axis=2, tiled=True
    ).astype(jnp.float32)
    normed = (
        embed_whole
        * lax.rsqrt(jnp.mean(embed_whole * embed_whole, -1, keepdims=True) + epsilon)
        * attn_gain
    ).astype(jnp.bfloat16)
    projected = jnp.einsum("sbd,dcf->sbcf", normed, w_qkv, preferred_element_type=jnp.float32)
    head_shape = (2, streams, heads_here, HD)
    positions = cache_lengths[None, :] + jnp.arange(2, dtype=jnp.int32)[:, None]
    queries = rotate(projected[:, :, 0].reshape(head_shape), positions).astype(jnp.bfloat16)
    new_keys = rotate(projected[:, :, 1].reshape(head_shape), positions).astype(jnp.bfloat16)
    new_values = projected[:, :, 2].reshape(head_shape).astype(jnp.bfloat16)
    new_kv = jnp.stack(
        [new_keys.reshape(2, streams, local_width), new_values.reshape(2, streams, local_width)]
    )
    inverse = HD ** (-0.5)
    key_rows = cache_keys.reshape(streams, slot_count, heads_here, HD)
    value_rows = cache_values.reshape(streams, slot_count, heads_here, HD)
    scores = (
        jnp.einsum("sbhe,bjhe->sbhj", queries, key_rows, preferred_element_type=jnp.float32)
        * inverse
    )
    slot_positions = seq_index * slot_count + jnp.arange(slot_count, dtype=jnp.int32)
    visible = (slot_positions[None, :] < cache_lengths[:, None])[None, :, None, :]
    local_max = jnp.max(jnp.where(visible, scores, -1e30), -1)
    weights = jnp.where(visible, jnp.exp(scores - local_max[..., None]), 0.0)
    local_sum = jnp.sum(weights, -1)
    local_out = jnp.einsum(
        "sbhj,bjhe->sbhe",
        weights,
        value_rows,
        preferred_element_type=jnp.float32,
        precision=lax.Precision.HIGHEST,
    )
    highest = lax.pmax(local_max, "seq")
    factor = jnp.exp(local_max - highest)
    cache_total, cache_out = lax.psum((local_sum * factor, local_out * factor[..., None]), "seq")
    fresh_scores = (
        jnp.einsum("sbhe,tbhe->sbht", queries, new_keys, preferred_element_type=jnp.float32)
        * inverse
    )
    allowed = (jnp.arange(2)[None, :] <= jnp.arange(2)[:, None])[:, None, None, :]
    fresh_max = jnp.max(jnp.where(allowed, fresh_scores, -1e30), -1)
    overall = jnp.maximum(highest, fresh_max)
    fresh_weights = jnp.where(allowed, jnp.exp(fresh_scores - overall[..., None]), 0.0)
    cache_scale = jnp.exp(highest - overall)
    denominator = cache_total * cache_scale + jnp.sum(fresh_weights, -1)
    numerator = cache_out * cache_scale[..., None] + jnp.einsum(
        "sbht,tbhe->sbhe",
        fresh_weights,
        new_values,
        preferred_element_type=jnp.float32,
        precision=lax.Precision.HIGHEST,
    )
    attended = (
        (numerator / denominator[..., None]).astype(jnp.bfloat16).reshape(2 * streams, local_width)
    )
    mixed_rows = jnp.dot(attended, w_out, preferred_element_type=jnp.float32).reshape(
        2, streams, model_width
    )
    mixed_local = lax.psum_scatter(mixed_rows, "tensor", scatter_dimension=2, tiled=True)
    hidden = (embed_local + mixed_local).astype(jnp.bfloat16)
    hidden_float = hidden.astype(jnp.float32)
    final_squares = lax.psum(jnp.sum(hidden_float * hidden_float, -1), "tensor")
    factor_rows = (
        lax.rsqrt(final_squares / model_width + epsilon) * (logit_gain / math.sqrt(model_width))
    ).reshape(2 * streams, 1)
    final_local = lax.dynamic_slice_in_dim(final_gain, tensor_index * local_width, local_width)
    gated_rows = (hidden_float * final_local).astype(jnp.bfloat16).reshape(2 * streams, local_width)
    partial_logits = lax.dot_general(
        gated_rows, embed_table, (((1,), (1,)), ((), ())), preferred_element_type=jnp.float32
    )
    shares = (
        lax.psum_scatter(partial_logits, "tensor", scatter_dimension=1, tiled=True) * factor_rows
    )
    share_max = jnp.max(shares, -1)
    share_sum = jnp.sum(jnp.exp(shares - share_max[:, None]), -1)
    vocab_max, vocab_sum = combined_all((share_max, share_sum), ("seq", "tensor"), pair_join)
    logprobs = shares - (vocab_max + jnp.log(vocab_sum))[:, None]
    return (hidden, new_kv, logprobs.reshape(2, streams, -1))


def solution(mesh):
    in_specs = (
        P(),
        P(),
        P("seq", "tensor"),
        P(),
        P(),
        P(None, None, "tensor"),
        P("tensor", None),
        P(None, "seq", "tensor"),
        P(None, "seq", "tensor"),
    )
    out_specs = (
        P(None, None, "tensor"),
        P(None, None, None, "tensor"),
        P(None, None, ("seq", "tensor")),
    )
    return jax.shard_map(body, mesh=mesh, in_specs=in_specs, out_specs=out_specs, check_vma=False)
```

profile of v0, /device:TPU:0, one launch (start us, length us, event | category | flops | bytes accessed | tf_op | source)
XLA Modules:
  0.0 251.6 jit_solution(10912633208323982474)
XLA Ops:
  7.2 0.8 compare_select_fusion
  8.1 0.7 compare_and_fusion
  9.5 0.7 broadcast_compare_fusion
  10.3 5.0 %gather_fusion = bf16[14,128]{1,0:T(8,128)(2,1)S(1)} fusion(bf16[32768,128]{1,0:T(8,128)(2,1)} %param.13, s32[1024]{0:T(1024)S(1)} %pad_clamp_fusion), kind=kCustom, calls=%fused_computation | custom fusion | bytes 7224 | tf_op jit(solution)/shard_map/gather | solution.py:65
  15.4 8.3 %psum.28 = bf16[2,7,128]{2,1,0:T(8,128)(2,1)S(1)} all-reduce(bf16[2,7,128]{2,1,0:T(8,128)(2,1)S(1)} %broadcast_select_fusion), channel_id=1, replica_groups=mesh['seq'=4,'tensor'=8] {'seq'}, use_global_device_ids=true, to_apply=%region_0.1 | all-reduce | flops 1792 | bytes 7168 | tf_op jit(solution)/shard_map/psum | solution.py:67
  23.7 26.4 %all_gather.15 = bf16[2,7,1024]{2,1,0:T(8,128)(2,1)S(1)} all-gather(bf16[2,7,128]{2,1,0:T(8,128)(2,1)S(1)} %psum.28), channel_id=1, replica_groups=mesh['seq'=4,'tensor'=8] {'tensor'}, dimensions={2}, use_global_device_ids=true | all-gather | bytes 32256 | tf_op jit(solution)/shard_map/all_gather | solution.py:70
  50.2 1.4 fusion.11
  51.8 0.8 select_reduce_fusion
  53.1 5.8 %pmax.7 = f32[2,7,1]{1,0,2:T(2,128)S(1)} all-reduce(f32[2,7,1]{1,0,2:T(2,128)S(1)} %bitcast.154), channel_id=1, replica_groups=mesh['seq'=4,'tensor'=8] {'seq'}, use_global_device_ids=true, to_apply=%region_3.4 | all-reduce | flops 14 | bytes 112 | tf_op jit(solution)/shard_map/pmax | solution.py:106
  59.5 2.7 %fusion.6 = f32[2,7,1,128]{3,0,1,2:T(2,128)S(1)} fusion(bf16[7,1280,128]{2,1,0:T(8,128)(2,1)} %param.19, f32[2,7,1,1280]{3,0,1,2:T(2,128)S(1)} %get-tuple-element.74, pred[7,1280]{1,0:T(8,128)(4,1)S(1)} %broadcast_compare_fusion, f32[2,7]{0,1:T(8,128)S(1)} %get-tuple-element.73, f32[2,7]{0,1:T(8,128)S(1)} %copy.54), kind=kOutput, calls=%fused_computation.12 | convolution fusion | flops 27562752 | bytes 2381680 | tf_op jit(solution)/shard_map/sbhj,bjhe->sbhe/dot_general | solution.py:99
  62.2 5.8 %all-reduce.3 = (f32[2,7,1,128]{3,0,1,2:T(2,128)S(1)}, f32[2,7,1]{1,0,2:T(2,128)S(1)}) all-reduce(f32[2,7,1,128]{3,0,1,2:T(2,128)S(1)} %fusion.6, f32[2,7,1]{1,0,2:T(2,128)S(1)} %get-tuple-element.70), channel_id=1, replica_groups=mesh['seq'=4,'tensor'=8] {'seq'}, use_global_device_ids=true, to_apply=%region_4.5 | all-reduce | flops 1806 | bytes 14448 | tf_op jit(solution)/shard_map/psum | solution.py:108
  68.4 0.8 fusion.13
  69.3 0.8 dynamic_slice.10
  70.1 53.2 %reduce-scatter.3.cloned.1.call-done = f32[2,7,128]{2,1,0:T(8,128)} async-done(((f32[2,7,1024]{2,1,0:T(8,128)}), f32[2,7,128]{2,1,0:T(8,128)}) %reduce-scatter.3.cloned.1.call-update) | async-done | bytes 7184 | tf_op jit(solution)/shard_map/reduce_scatter | solution.py:132
  123.3 0.8 fusion.33
  124.1 7.0 %fusion.62 = f32[14,32768]{1,0:T(8,128)} fusion(bf16[14,128]{1,0:T(8,128)(2,1)S(1)} %reshape.218, bf16[32768,128]{1,0:T(8,128)(2,1)} %param.13), kind=kOutput, calls=%fused_computation.106 | convolution fusion | flops 117440512 | bytes 10227200 | tf_op jit(solution)/shard_map/dot_general | solution.py:141
  131.8 19.6 %psum.31 = f32[2,7]{1,0:T(2,128)S(1)} all-reduce(f32[2,7]{1,0:T(2,128)S(1)} %get-tuple-element.58), channel_id=1, replica_groups=mesh['seq'=4,'tensor'=8] {'tensor'}, use_global_device_ids=true, to_apply=%region_12.13 | all-reduce | flops 14 | bytes 112 | tf_op jit(solution)/shard_map/psum | solution.py:135
  152.1 46.9 %reduce-scatter.5.cloned.1.call-done = f32[14,4096]{1,0:T(8,128)} async-done(((f32[14,32768]{1,0:T(8,128)}), f32[14,4096]{1,0:T(8,128)}) %reduce-scatter.5.cloned.1.call-update) | async-done | bytes 229392 | tf_op jit(solution)/shard_map/reduce_scatter | solution.py:145
  199.0 1.2 multiply_reduce_fusion
  200.4 1.2 exponential_reduce_fusion
  201.9 39.3 %all-reduce.2 = (f32[448]{0:T(512)S(1)}, f32[448]{0:T(512)S(1)}) all-reduce(f32[448]{0:T(512)S(1)} %dynamic-update-slice, f32[448]{0:T(512)S(1)} %dynamic-update-slice.1), channel_id=2, replica_groups=mesh['seq'=4,'tensor'=8] {'seq','tensor'}, use_global_device_ids=true, to_apply=%add | all-reduce | flops 896 | bytes 7168
  241.6 1.2 while.12
  242.8 1.0 multiply_subtract_fusion
  243.9 0.9 copy.69
  (85 shorter events, 5.7 us)
Async XLA Ops:
  7.2 44.7 %copy-start = (bf16[7,1280,128]{2,1,0:T(8,128)(2,1)S(1)}, bf16[7,1280,128]{2,1,0:T(8,128)(2,1)}, u32[]{:S(2)}) copy-start(bf16[7,1280,128]{2,1,0:T(8,128)(2,1)} %param.18) | copy-start | bytes 6881284
  7.2 116.1 %reduce-scatter.3.cloned.1.call-start = ((), (), s32[]{:S(2)}) async-start(), calls=%async_computation.2 | async-start | bytes 73728 | tf_op jit(solution)/shard_map/reduce_scatter | solution.py:132
  51.8 16.6 %copy-start.1 = (bf16[128,1024]{1,0:T(8,128)(2,1)S(1)}, bf16[128,1024]{1,0:T(8,128)(2,1)}, u32[]{:S(2)}) copy-start(bf16[128,1024]{1,0:T(8,128)(2,1)} %param.17) | copy-start | bytes 786436
  69.3 129.8 %reduce-scatter.5.cloned.1.call-start = ((), (), s32[]{:S(2)}) async-start(), calls=%async_computation.3 | async-start | bytes 2359296 | tf_op jit(solution)/shard_map/reduce_scatter | solution.py:145
Sparse Core Ops, SparseCore 0:
  69.4 53.8 reduce-scatter.2
  131.3 67.7 reduce-scatter.4
where the time goes:
time: 252 us
  blocking collectives  105 us (42%)
  waiting for transfers between devices  100 us (40%)
  between operations  14.2 us (6%)
  matrix products  13 us (5%)
  local copies, waits for them, and re-layouts  9.57 us (4%)
  other arithmetic  8.84 us (4%)
    reduce_scatter x1, waiting for transfers between devices, body(): lax.psum_scatter(mixed_rows, 'tensor', scatter_dimension=2, tiled=True)  53.2 us
    reduce_scatter x1, waiting for transfers between devices, body(): lax.psum_scatter(partial_logits, 'tensor', scatter_dimension=1, tiled=True)  46.9 us
    unnamed x1, blocking collectives  39.3 us
    all_gather x1, blocking collectives, body(): lax.all_gather(embed_local.astype(jnp.bfloat16), 'tensor', axis=2, tiled=...  26.4 us
    psum x1, blocking collectives, body(): final_squares = lax.psum(jnp.sum(hidden_float * hidden_float, -1), 'tensor')  19.6 us
    psum x1, blocking collectives, body(): lax.psum(picked.astype(jnp.float32).astype(jnp.bfloat16), 'seq')  8.35 us
    dot_general x1, matrix products, body(): lax.dot_general(gated_rows, embed_table, (((1,), (1,)), ((), ())), prefer...  7.03 us
    pmax x1, blocking collectives, body(): highest = lax.pmax(local_max, 'seq')  5.85 us
  transfers between devices with their start and end apart: 2, of which 2 were waited for; matrix products, arithmetic and copies ran while one was open for 1% of the time, Pallas kernels for 0%

commit v1 on v0

--- a/solution.py
+++ b/solution.py
@@ -7,6 +7,18 @@
 HD = 128
 epsilon = 1e-05
 logit_gain = 2.0
+
+
+def gather_by_bits(array, axis, dim):
+    ways, here = (lax.axis_size(axis), lax.axis_index(axis))
+    grown, reach = (array, 1)
+    while reach < ways:
+        theirs = lax.ppermute(grown, axis, [(d, d ^ reach) for d in range(ways)])
+        mine_first = jnp.concatenate([grown, theirs], axis=dim)
+        theirs_first = jnp.concatenate([theirs, grown], axis=dim)
+        grown = jnp.where(here & reach == 0, mine_first, theirs_first)
+        reach = 2 * reach
+    return grown
 
 
 def combined_all(value, axis, join):
@@ -67,9 +79,7 @@
     embed_local = lax.psum(picked.astype(jnp.float32).astype(jnp.bfloat16), "seq").astype(
         jnp.float32
     )
-    embed_whole = lax.all_gather(
-        embed_local.astype(jnp.bfloat16), "tensor", axis=2, tiled=True
-    ).astype(jnp.float32)
+    embed_whole = gather_by_bits(embed_local.astype(jnp.bfloat16), "tensor", 2).astype(jnp.float32)
     normed = (
         embed_whole
         * lax.rsqrt(jnp.mean(embed_whole * embed_whole, -1, keepdims=True) + epsilon)

time: 252 us -> 238 us (0.944)
  blocking collectives: 105 us -> 79 us
  waiting for transfers between devices: 100 us -> 107 us
  starting transfers between devices: 0.08 us -> 5.89 us
    all_gather x1 -> x0, blocking collectives: 26.4 us -> none  [body(): lax.all_gather(embed_local.astype(jnp.bfloat16), 'tensor', axis=2, tiled=...]
    ppermute x0 -> x3, starting transfers between devices: none -> 5.81 us  [gather_by_bits(): theirs = lax.ppermute(grown, axis, [(d, d ^ reach) for d in range(ways)])]
    ppermute x0 -> x3, waiting for transfers between devices: none -> 4.8 us  [gather_by_bits(): theirs = lax.ppermute(grown, axis, [(d, d ^ reach) for d in range(ways)])]
  transfers between devices with their start and end apart: 2 -> 5, of which waited for: 2 -> 5; matrix products, arithmetic and copies ran while one was open for 1% -> 1% of each run, Pallas kernels for 0% -> 0%
where the time goes in v1:
time: 238 us; the launch traced here: 237 us
  waiting for transfers between devices  107 us (45%)
  blocking collectives  79 us (33%)
  between operations  14.2 us (6%)
  matrix products  13 us (5%)
  local copies, waits for them, and re-layouts  9.57 us (4%)
  other arithmetic  8.85 us (4%)
  starting transfers between devices  5.89 us (2%)
    reduce_scatter x1, waiting for transfers between devices, body(): lax.psum_scatter(mixed_rows, 'tensor', scatter_dimension=2, tiled=True)  55.2 us
    reduce_scatter x1, waiting for transfers between devices, body(): lax.psum_scatter(partial_logits, 'tensor', scatter_dimension=1, tiled=True)  46.5 us
    unnamed x1, blocking collectives  39.5 us
    psum x1, blocking collectives, body(): final_squares = lax.psum(jnp.sum(hidden_float * hidden_float, -1), 'tensor')  19.6 us
    psum x1, blocking collectives, body(): lax.psum(picked.astype(jnp.float32).astype(jnp.bfloat16), 'seq')  8.35 us
    dot_general x1, matrix products, body(): lax.dot_general(gated_rows, embed_table, (((1,), (1,)), ((), ())), prefer...  7.03 us
    psum x1, blocking collectives, body(): lax.psum((local_sum * factor, local_out * factor[..., None]), 'seq')  5.85 us
    ppermute x3, starting transfers between devices, gather_by_bits(): theirs = lax.ppermute(grown, axis, [(d, d ^ reach) for d in range(ways)])  5.81 us
  transfers between devices with their start and end apart: 5, of which 5 were waited for; matrix products, arithmetic and copies ran while one was open for 1% of the time, Pallas kernels for 0%

profile of v1, /device:TPU:0, one launch (start us, length us, event | category | flops | bytes accessed | tf_op | source)
XLA Modules:
  0.0 237.5 jit_solution(908603169623369550)
XLA Ops:
  7.2 0.8 compare_select_fusion
  8.8 5.0 %gather_fusion = bf16[14,128]{1,0:T(8,128)(2,1)S(1)} fusion(bf16[32768,128]{1,0:T(8,128)(2,1)} %param.13, s32[1024]{0:T(1024)S(1)} %pad_clamp_fusion), kind=kCustom, calls=%fused_computation | custom fusion | bytes 7224 | tf_op jit(solution)/shard_map/gather | solution.py:77
  14.0 8.3 %psum.28 = bf16[2,7,128]{2,1,0:T(8,128)(2,1)S(1)} all-reduce(bf16[2,7,128]{2,1,0:T(8,128)(2,1)S(1)} %broadcast_select_fusion), channel_id=1, replica_groups=mesh['seq'=4,'tensor'=8] {'seq'}, use_global_device_ids=true, to_apply=%region_0.1 | all-reduce | flops 1792 | bytes 7168 | tf_op jit(solution)/shard_map/psum | solution.py:79
  22.3 1.6 collective-permute-start
  26.0 1.6 collective-permute-start.1
  27.6 2.1 collective-permute-done.1
  29.6 2.7 %collective-permute-start.2 = (bf16[2,7,512]{2,1,0:T(8,128)(2,1)S(1)}, bf16[2,7,512]{2,1,0:T(8,128)(2,1)S(1)}, u32[]{:S(2)}, u32[]{:S(2)}) collective-permute-start(bf16[2,7,512]{2,1,0:T(8,128)(2,1)S(1)} %maximum_select_fusion.1), channel_id=1, source_target_pairs={{0,4},{1,5},{2,6},{3,7},{4,0},{5,1},{6,2},{7,3},{8,12},{9,13},{10,... | collective-permute-start | bytes 43016 | tf_op jit(solution)/shard_map/ppermute | solution.py:16
  32.3 2.0 collective-permute-done.2
  34.5 1.4 fusion.11
  36.1 0.8 select_reduce_fusion
  37.3 5.7 %pmax.7 = f32[2,7,1]{1,0,2:T(2,128)S(1)} all-reduce(f32[2,7,1]{1,0,2:T(2,128)S(1)} %bitcast.154), channel_id=1, replica_groups=mesh['seq'=4,'tensor'=8] {'seq'}, use_global_device_ids=true, to_apply=%region_3.4 | all-reduce | flops 14 | bytes 112 | tf_op jit(solution)/shard_map/pmax | solution.py:116
  43.6 2.7 %fusion.6 = f32[2,7,1,128]{3,0,1,2:T(2,128)S(1)} fusion(bf16[7,1280,128]{2,1,0:T(8,128)(2,1)} %param.19, f32[2,7,1,1280]{3,0,1,2:T(2,128)S(1)} %get-tuple-element.74, pred[7,1280]{1,0:T(8,128)(4,1)S(1)} %broadcast_compare_fusion, f32[2,7]{0,1:T(8,128)S(1)} %get-tuple-element.73, f32[2,7]{0,1:T(8,128)S(1)} %copy.54), kind=kOutput, calls=%fused_computation.12 | convolution fusion | flops 27562752 | bytes 2381680 | tf_op jit(solution)/shard_map/sbhj,bjhe->sbhe/dot_general | solution.py:109
  46.4 5.8 %all-reduce.3 = (f32[2,7,1,128]{3,0,1,2:T(2,128)S(1)}, f32[2,7,1]{1,0,2:T(2,128)S(1)}) all-reduce(f32[2,7,1,128]{3,0,1,2:T(2,128)S(1)} %fusion.6, f32[2,7,1]{1,0,2:T(2,128)S(1)} %get-tuple-element.70), channel_id=1, replica_groups=mesh['seq'=4,'tensor'=8] {'seq'}, use_global_device_ids=true, to_apply=%region_4.5 | all-reduce | flops 1806 | bytes 14448 | tf_op jit(solution)/shard_map/psum | solution.py:118
  52.6 0.8 fusion.13
  54.2 55.2 %reduce-scatter.3.cloned.1.call-done = f32[2,7,128]{2,1,0:T(8,128)} async-done(((f32[2,7,1024]{2,1,0:T(8,128)}), f32[2,7,128]{2,1,0:T(8,128)}) %reduce-scatter.3.cloned.1.call-update) | async-done | bytes 7184 | tf_op jit(solution)/shard_map/reduce_scatter | solution.py:142
  110.2 7.0 %fusion.63 = f32[14,32768]{1,0:T(8,128)} fusion(bf16[14,128]{1,0:T(8,128)(2,1)S(1)} %reshape.218, bf16[32768,128]{1,0:T(8,128)(2,1)} %param.13), kind=kOutput, calls=%fused_computation.110 | convolution fusion | flops 117440512 | bytes 10227200 | tf_op jit(solution)/shard_map/dot_general | solution.py:151
  118.0 19.6 %psum.31 = f32[2,7]{1,0:T(2,128)S(1)} all-reduce(f32[2,7]{1,0:T(2,128)S(1)} %get-tuple-element.58), channel_id=1, replica_groups=mesh['seq'=4,'tensor'=8] {'tensor'}, use_global_device_ids=true, to_apply=%region_12.13 | all-reduce | flops 14 | bytes 112 | tf_op jit(solution)/shard_map/psum | solution.py:145
  138.2 46.5 %reduce-scatter.5.cloned.1.call-done = f32[14,4096]{1,0:T(8,128)} async-done(((f32[14,32768]{1,0:T(8,128)}), f32[14,4096]{1,0:T(8,128)}) %reduce-scatter.5.cloned.1.call-update) | async-done | bytes 229392 | tf_op jit(solution)/shard_map/reduce_scatter | solution.py:155
  184.8 1.2 multiply_reduce_fusion
  186.2 1.2 exponential_reduce_fusion
  187.6 39.5 %all-reduce.2 = (f32[448]{0:T(512)S(1)}, f32[448]{0:T(512)S(1)}) all-reduce(f32[448]{0:T(512)S(1)} %dynamic-update-slice, f32[448]{0:T(512)S(1)} %dynamic-update-slice.1), channel_id=2, replica_groups=mesh['seq'=4,'tensor'=8] {'seq','tensor'}, use_global_device_ids=true, to_apply=%add | all-reduce | flops 896 | bytes 7168
  227.4 1.2 while.12
  228.7 1.0 multiply_subtract_fusion
  229.8 0.9 copy.69
  (92 shorter events, 9.4 us)
Async XLA Ops:
  7.2 28.9 %copy-start = (bf16[7,1280,128]{2,1,0:T(8,128)(2,1)S(1)}, bf16[7,1280,128]{2,1,0:T(8,128)(2,1)}, u32[]{:S(2)}) copy-start(bf16[7,1280,128]{2,1,0:T(8,128)(2,1)} %param.18) | copy-start | bytes 6881284
  7.2 102.2 %reduce-scatter.3.cloned.1.call-start = ((), (), s32[]{:S(2)}) async-start(), calls=%async_computation.2 | async-start | bytes 73728 | tf_op jit(solution)/shard_map/reduce_scatter | solution.py:142
  22.3 3.7 %collective-permute-start = (bf16[2,7,128]{2,1,0:T(8,128)(2,1)S(1)}, bf16[2,7,128]{2,1,0:T(8,128)(2,1)S(1)}, u32[]{:S(2)}, u32[]{:S(2)}) collective-permute-start(bf16[2,7,128]{2,1,0:T(8,128)(2,1)S(1)} %psum.28), channel_id=1, source_target_pairs={{0,1},{1,0},{2,3},{3,2},{4,5},{5,4},{6,7},{7,6},{8,9},{9,8},{10,11... | collective-permute-start | bytes 10760 | tf_op jit(solution)/shard_map/ppermute | solution.py:16
  26.0 3.7 %collective-permute-start.1 = (bf16[2,7,256]{2,1,0:T(8,128)(2,1)S(1)}, bf16[2,7,256]{2,1,0:T(8,128)(2,1)S(1)}, u32[]{:S(2)}, u32[]{:S(2)}) collective-permute-start(bf16[2,7,256]{2,1,0:T(8,128)(2,1)S(1)} %maximum_select_fusion.2), channel_id=1, source_target_pairs={{0,2},{1,3},{2,0},{3,1},{4,6},{5,7},{6,4},{7,5},{8,10},{9,11},{10,... | collective-permute-start | bytes 21512 | tf_op jit(solution)/shard_map/ppermute | solution.py:16
  29.6 4.7 %collective-permute-start.2 = (bf16[2,7,512]{2,1,0:T(8,128)(2,1)S(1)}, bf16[2,7,512]{2,1,0:T(8,128)(2,1)S(1)}, u32[]{:S(2)}, u32[]{:S(2)}) collective-permute-start(bf16[2,7,512]{2,1,0:T(8,128)(2,1)S(1)} %maximum_select_fusion.1), channel_id=1, source_target_pairs={{0,4},{1,5},{2,6},{3,7},{4,0},{5,1},{6,2},{7,3},{8,12},{9,13},{10,... | collective-permute-start | bytes 43016 | tf_op jit(solution)/shard_map/ppermute | solution.py:16
  36.1 16.5 %copy-start.1 = (bf16[128,1024]{1,0:T(8,128)(2,1)S(1)}, bf16[128,1024]{1,0:T(8,128)(2,1)}, u32[]{:S(2)}) copy-start(bf16[128,1024]{1,0:T(8,128)(2,1)} %param.17) | copy-start | bytes 786436
  53.4 131.4 %reduce-scatter.5.cloned.1.call-start = ((), (), s32[]{:S(2)}) async-start(), calls=%async_computation.3 | async-start | bytes 2359296 | tf_op jit(solution)/shard_map/reduce_scatter | solution.py:155
Sparse Core Ops, SparseCore 0:
  53.5 55.8 reduce-scatter.2
  117.4 67.3 reduce-scatter.4
